TPU v7x, 128 devices: a whole 4x4x4 slice. The times are simulated.
128 devices in a mesh: island: 8 (over x_lo, z), shard: 16 (over y, x_hi, core).
Axes of the slice: x: 4 (x_hi: 2, x_lo: 2; x = x_hi * 2 + x_lo), y: 4, z: 4, core: 2. Of those that a mesh axis runs over, the one named last changes fastest.
Arguments:
- weight_master: float32 [4096, 4096], P('island', 'shard'), may hold values from -6 to 6
- gain_master: float32 [4096], P(('shard', 'island')), may hold values from 0.5 to 1.5
- weight_moment: float32 [4096, 4096], P('island', 'shard'), may hold values from -0.3 to 0.3
- gain_moment: float32 [4096], P(('shard', 'island')), may hold values from -0.3 to 0.3
- attended: bfloat16 [8, 2, 1536, 4096], P('island', None, 'shard'), may hold values from -6 to 6
- stream: bfloat16 [8, 2, 1536, 4096], P('island', None, None, 'shard'), may hold values from -6 to 6
- targets: bfloat16 [8, 2, 1536, 4096], P('island', None, None, 'shard'), may hold values from -6 to 6
Outputs:
- weight_updated: float32 [4096, 4096], P('island', 'shard')
- gain_updated: float32 [4096], P(('shard', 'island'))
- weight_velocity: float32 [4096, 4096], P('island', 'shard')
- gain_velocity: float32 [4096], P(('shard', 'island'))
All inputs are finite; a program needn't handle non-finite values.
Results may differ from a plain program's by a relative error of at most 0.0066.
Values may be sent and summed in bfloat16 or wider, within the bound.
No kernel may reach another device: no remote copies, remote signals or barrier semaphores. Data moves between devices by JAX's collectives and lax.ppermute only.
A program may use at most 192 MiB of HBM per device.

v0:
```python
import jax
import jax.numpy as jnp
from jax import lax
from jax.sharding import Mesh
from jax.sharding import PartitionSpec as P

D = 4096
STEPS = 2
SHARD = ("shard_0", "shard_1", "shard_2")
SHARD_ISLAND = ("shard_0", "shard_1", "shard_2", "island")
norm_epsilon = 1e-05
inner_rate = 0.05
beta_one = 0.9
beta_two = 0.95
adam_epsilon = 0.3
decay_rate = 0.1
outer_rate = 0.7
outer_momentum = 0.9


def joined_along(blocks, dim):
    shape = list(blocks.shape[1:])
    shape[dim] *= blocks.shape[0]
    return jnp.moveaxis(blocks, 0, dim).reshape(shape)


def gather_packed(arrays, axis, dims):
    vector = jnp.concatenate([a.reshape(-1) for a in arrays])
    lines, at, gathered = (lax.all_gather(vector, axis), 0, [])
    for a, dim in zip(arrays, dims):
        blocks = lines[:, at : at + a.size].reshape(-1, *a.shape)
        gathered.append(joined_along(blocks, dim))
        at += a.size
    return tuple(gathered)


def one_axis_at_a_time(value, axes):
    for axis in axes:
        value = lax.psum(value, axis)
    return value


def copy_for_each(value, axis):
    copies = jnp.broadcast_to(value, (lax.axis_size(axis), *value.shape))
    return lax.all_to_all(copies, axis, split_axis=0, concat_axis=0, tiled=True)


def taken_together(value, axis):
    everything = copy_for_each(value, axis)
    return jnp.sum(everything, axis=0)


def split_up(value, dim, size):
    shape = value.shape
    blocks = value.reshape(*shape[:dim], size, shape[dim] // size, *shape[dim + 1 :])
    return jnp.moveaxis(blocks, dim, 0)


def sent_and_summed(value, axis, dim):
    blocks = split_up(value, dim, lax.axis_size(axis))
    arrived = lax.all_to_all(blocks, axis, split_axis=0, concat_axis=0, tiled=True)
    return arrived.astype(jnp.float32).sum(axis=0)


def optimizer_update(param, gradient, first, second, number, decay):
    first = beta_one * first + (1.0 - beta_one) * gradient
    second = beta_two * second + (1.0 - beta_two) * gradient * gradient
    first_hat = first / (1.0 - beta_one**number)
    second_hat = second / (1.0 - beta_two**number)
    param = param - inner_rate * (first_hat / (jnp.sqrt(second_hat) + adam_epsilon) + decay * param)
    return (param, first, second)


def per_device(weight_master, gain_master, weight_moment, gain_moment, attended, stream, targets):
    islands = lax.axis_size("island")
    width_scale = D ** (-0.5)
    starts = gather_packed(
        (weight_master.astype(jnp.bfloat16), gain_master.astype(jnp.bfloat16)), "island", (0, 0)
    )
    weight_anchor = starts[0].astype(jnp.float32)
    gain_anchor = starts[1].astype(jnp.float32)
    weight = weight_anchor
    gain = gain_anchor
    weight_first = jnp.zeros_like(weight)
    weight_second = jnp.zeros_like(weight)
    gain_first = jnp.zeros_like(gain)
    gain_second = jnp.zeros_like(gain)
    for inner_step in range(STEPS):
        number = inner_step + 1
        rows_full = lax.all_gather(attended[0][inner_step], SHARD, axis=0, tiled=True)
        weight_low = weight.astype(jnp.bfloat16)
        projected = jnp.dot(rows_full, weight_low, preferred_element_type=jnp.float32) * width_scale
        residual = stream[0][inner_step].astype(jnp.float32) + projected
        squares = one_axis_at_a_time(jnp.sum(residual * residual, axis=1), SHARD)
        inverse = lax.rsqrt(squares / D + norm_epsilon)[:, None]
        normed = residual * inverse * gain
        loss_low = (normed - targets[0][inner_step].astype(jnp.float32)).astype(jnp.bfloat16)
        loss_grad = lax.optimization_barrier(loss_low).astype(jnp.float32)
        scaled = loss_grad * gain
        slope = taken_together(jnp.sum(scaled * residual, axis=1), SHARD)[:, None]
        residual_grad = (
            inverse * scaled - residual * inverse * inverse * inverse * slope / D
        ).astype(jnp.bfloat16)
        weight_grad = (
            jnp.einsum("td,tf->df", rows_full, residual_grad, preferred_element_type=jnp.float32)
            * width_scale
        )
        gain_grad = jnp.sum(loss_grad * residual * inverse, axis=0)
        weight, weight_first, weight_second = optimizer_update(
            weight, weight_grad, weight_first, weight_second, number, decay_rate
        )
        gain, gain_first, gain_second = optimizer_update(
            gain, gain_grad, gain_first, gain_second, number, 0.0
        )
    weight_summed, gain_summed = (
        sent_and_summed((weight_anchor - weight).astype(jnp.bfloat16), "island", 0),
        sent_and_summed((gain_anchor - gain).astype(jnp.bfloat16), "island", 0),
    )
    weight_pseudo = weight_summed / islands
    gain_pseudo = gain_summed / islands
    weight_velocity = outer_momentum * weight_moment + weight_pseudo
    gain_velocity = outer_momentum * gain_moment + gain_pseudo
    weight_updated = weight_master - outer_rate * (weight_pseudo + outer_momentum * weight_velocity)
    gain_updated = gain_master - outer_rate * (gain_pseudo + outer_momentum * gain_velocity)
    return (weight_updated, gain_updated, weight_velocity, gain_velocity)


def solution(mesh):
    torus = Mesh(
        mesh.devices.reshape(mesh.shape["island"], 4, 2, 2),
        ("island", "shard_0", "shard_1", "shard_2"),
    )
    return jax.shard_map(
        per_device,
        mesh=torus,
        in_specs=(
            P("island", SHARD),
            P(SHARD_ISLAND),
            P("island", SHARD),
            P(SHARD_ISLAND),
            P("island", None, SHARD, None),
            P("island", None, None, SHARD),
            P("island", None, None, SHARD),
        ),
        out_specs=(P("island", SHARD), P(SHARD_ISLAND), P("island", SHARD), P(SHARD_ISLAND)),
        check_vma=False,
    )
```

profile of v0, /device:TPU:1, one launch (start us, length us, event | category | flops | bytes accessed | tf_op | source)
XLA Modules:
  0.0 327.8 jit_solution(17486455540308748270)
XLA Ops:
  8.0 0.0 all-reduce.3.cloned.1.call-start
  8.0 1.1 convert_bitcast_fusion
  9.1 0.2 copy.77
  9.3 0.7 convert_element_type.86
  10.0 1.2 dynamic-slice
  11.9 0.2 broadcast.157
  12.1 2.6 dynamic-update-slice
  14.8 1.3 copy-done
  16.1 0.0 all-gather.6.cloned.1.call-start
  16.2 2.8 fusion.91
  19.0 0.0 all-gather.8.cloned.1.call-start
  19.0 0.5 all-gather.8.cloned.1.call-update
  19.6 0.1 fusion.90
  19.7 1.2 copy.72
  20.9 1.5 fusion.89
  22.3 1.2 copy.73
  23.5 1.2 copy.74
  24.7 0.3 copy.75
  24.9 119.6 %all-reduce.3.cloned.1.call-done = bf16[1048832]{0:T(1024)(128)(2,1)} async-done(((bf16[1048832]{0:T(1024)(128)(2,1)}), bf16[1048832]{0:T(1024)(128)(2,1)}) %all-reduce.3.cloned.1.call-update) | async-done | bytes 2097680
  144.5 4.1 %reshape.82 = bf16[8,131104]{1,0:T(8,128)(2,1)S(1)} reshape(bf16[1048832]{0:T(1024)(128)(2,1)} %all-reduce.3.cloned.1.call-done) | data formatting | bytes 4195328 | tf_op jit(solution)/shard_map/all_gather | solution.py:29
  148.6 1.4 slice.38
  150.0 3.9 %reshape_reshape.3 = bf16[4096,256]{1,0:T(8,128)(2,1)} reshape(bf16[8,131072]{1,0:T(8,128)(2,1)} %slice.38) | data formatting | bytes 4194304 | tf_op jit(solution)/shard_map/reshape;reshape | solution.py:24
  154.0 0.1 reshape.78
  154.0 4.2 %copy.55 = bf16[4096,256]{0,1:T(8,128)(2,1)} copy(bf16[4096,256]{1,0:T(8,128)(2,1)} %reshape_reshape.3) | data formatting | bytes 4194304 | tf_op jit(solution)/shard_map/reshape;reshape | solution.py:24
  158.2 10.2 %multiply_reduce_fusion.1 = (f32[1536]{0:T(1024)S(1)}, f32[1536,256]{0,1:T(8,128)}) fusion(bf16[4096,256]{1,0:T(8,128)(2,1)} %reshape_reshape.3, bf16[1,1,1536,4096]{3,2,1,0:T(8,128)(2,1)} %all-gather.6.cloned.1.call-done, bf16[1,1,1536,256]{2,3,1,0:T(8,128)(2,1)} %copy.72), kind=kOutput, calls=%fused_computation.56 | convolution fusion | flops 3223190016 | bytes 17045504 | tf_op jit(solution)/shard_map/dot_general | solution.py:92
  168.5 9.4 %psum.42 = f32[1536]{0:T(1024)S(1)} all-reduce(f32[1536]{0:T(1024)S(1)} %get-tuple-element.34), channel_id=1, replica_groups=mesh['island'=8,'shard_0'=4,'shard_1'=2,'shard_2'=2] {'shard_0'}, use_global_device_ids=true, to_apply=%region_1.0 | all-reduce | flops 1536 | bytes 12288 | tf_op jit(solution)/shard_map/psum | solution.py:39
  177.9 6.0 %psum.43 = f32[1536]{0:T(1024)S(1)} all-reduce(f32[1536]{0:T(1024)S(1)} %psum.42), channel_id=1, replica_groups=mesh['island'=8,'shard_0'=4,'shard_1'=2,'shard_2'=2] {'shard_1'}, use_global_device_ids=true, to_apply=%region_2.0 | all-reduce | flops 1536 | bytes 12288 | tf_op jit(solution)/shard_map/psum | solution.py:39
  183.9 9.4 %psum.44 = f32[1536]{0:T(1024)S(1)} all-reduce(f32[1536]{0:T(1024)S(1)} %psum.43), channel_id=1, replica_groups=mesh['island'=8,'shard_0'=4,'shard_1'=2,'shard_2'=2] {'shard_2'}, use_global_device_ids=true, to_apply=%region_3.0 | all-reduce | flops 1536 | bytes 12288 | tf_op jit(solution)/shard_map/psum | solution.py:39
  193.4 2.0 fusion.54
  195.4 0.1 copy-done.2
  195.5 0.6 fusion.50
  196.1 0.3 copy-done.4
  196.4 0.7 broadcast_in_dim.4
  197.1 4.8 %all-to-all-start = ((f32[16,1,1536]{2,1,0:T(1,128)}), f32[16,1,1536]{2,1,0:T(1,128)S(1)}, u32[]{:S(2)}, u32[]{:S(2)}) async-start(f32[16,1,1536]{2,1,0:T(1,128)} %broadcast_in_dim.4), calls=%async_computation | async-start | bytes 196608 | tf_op jit(solution)/shard_map/all_to_all | solution.py:45
  201.9 0.1 reduce_sum.102
  201.9 7.2 %all-to-all-done = f32[16,1,1536]{2,1,0:T(1,128)S(1)} async-done(((f32[16,1,1536]{2,1,0:T(1,128)}), f32[16,1,1536]{2,1,0:T(1,128)S(1)}, u32[]{:S(2)}, u32[]{:S(2)}) %all-to-all-start) | async-done | bytes 98336 | tf_op jit(solution)/shard_map/all_to_all | solution.py:45
  209.2 0.1 reduce_sum.96
  209.3 10.9 %fusion.4 = f32[256,4096]{1,0:T(8,128)} fusion(bf16[1,1,1536,4096]{3,2,1,0:T(8,128)(2,1)} %all-gather.6.cloned.1.call-done, bf16[1536,256]{0,1:T(8,128)(2,1)} %copy-done.4, f32[1536,256]{0,1:T(8,128)} %get-tuple-element.35, f32[1536]{0:T(1024)S(1)} %reduce_sum.96, f32[256]{0:T(256)S(1)} %reshape.78, f32[1536]{0:T(1024)S(1)} %add_rsqrt_fusion.1), kind=kOutput, calls=%fused_computation.4 | convolution fusion | flops 3225157632 | bytes 19149824 | tf_op jit(solution)/shard_map/td,tf->df/dot_general | solution.py:105
  220.2 13.4 %multiply_reduce_fusion = (f32[1536]{0:T(1024)S(1)}, f32[1536,256]{0,1:T(8,128)}) fusion(bf16[1,1,1536,4096]{3,2,1,0:T(8,128)(2,1)} %all-gather.8.cloned.1.call-done, f32[256,4096]{1,0:T(8,128)} %fusion.4, bf16[4096,256]{0,1:T(8,128)(2,1)} %copy.55, bf16[1,1,1536,256]{2,3,1,0:T(8,128)(2,1)} %copy.74), kind=kOutput, calls=%fused_computation.55 | convolution fusion | flops 3235772928 | bytes 21239808 | tf_op jit(solution)/shard_map/dot_general | solution.py:92
  233.6 7.0 %psum.45 = f32[1536]{0:T(1024)S(1)} all-reduce(f32[1536]{0:T(1024)S(1)} %get-tuple-element.36), channel_id=1, replica_groups=mesh['island'=8,'shard_0'=4,'shard_1'=2,'shard_2'=2] {'shard_0'}, use_global_device_ids=true, to_apply=%region_7.0 | all-reduce | flops 1536 | bytes 12288 | tf_op jit(solution)/shard_map/psum | solution.py:39
  240.6 5.4 %psum.46 = f32[1536]{0:T(1024)S(1)} all-reduce(f32[1536]{0:T(1024)S(1)} %psum.45), channel_id=1, replica_groups=mesh['island'=8,'shard_0'=4,'shard_1'=2,'shard_2'=2] {'shard_1'}, use_global_device_ids=true, to_apply=%region_8.0 | all-reduce | flops 1536 | bytes 12288 | tf_op jit(solution)/shard_map/psum | solution.py:39
  246.0 5.7 %psum.47 = f32[1536]{0:T(1024)S(1)} all-reduce(f32[1536]{0:T(1024)S(1)} %psum.46), channel_id=1, replica_groups=mesh['island'=8,'shard_0'=4,'shard_1'=2,'shard_2'=2] {'shard_2'}, use_global_device_ids=true, to_apply=%region_9.0 | all-reduce | flops 1536 | bytes 12288 | tf_op jit(solution)/shard_map/psum | solution.py:39
  251.6 1.8 fusion.53
  253.5 0.0 copy-done.1
  253.5 0.6 fusion.52
  254.2 0.2 copy-done.3
  254.4 0.1 reduce_sum.104
  254.5 0.7 broadcast_in_dim.5
  255.2 3.6 %all-to-all-start.1 = ((f32[16,1,1536]{2,1,0:T(1,128)}), f32[16,1,1536]{2,1,0:T(1,128)S(1)}, u32[]{:S(2)}, u32[]{:S(2)}) async-start(f32[16,1,1536]{2,1,0:T(1,128)} %broadcast_in_dim.5), calls=%async_computation.1 | async-start | bytes 196608 | tf_op jit(solution)/shard_map/all_to_all | solution.py:45
  258.8 0.6 copy.66
  259.4 6.8 %all-to-all-done.1 = f32[16,1,1536]{2,1,0:T(1,128)S(1)} async-done(((f32[16,1,1536]{2,1,0:T(1,128)}), f32[16,1,1536]{2,1,0:T(1,128)S(1)}, u32[]{:S(2)}, u32[]{:S(2)}) %all-to-all-start.1) | async-done | bytes 98336 | tf_op jit(solution)/shard_map/all_to_all | solution.py:45
  266.2 4.3 %all-to-all-start.3 = ((bf16[8,1,32]{2,1,0:T(2,128)(2,1)}), bf16[8,1,32]{2,1,0:T(2,128)(2,1)S(1)}, u32[]{:S(2)}, u32[]{:S(2)}) async-start(bf16[8,1,32]{2,1,0:T(2,128)(2,1)} %copy.66), calls=%async_computation.3 | async-start | bytes 8192 | tf_op jit(solution)/shard_map/all_to_all | solution.py:61
  270.5 0.1 reduce_sum.100
  270.6 14.3 %fusion.10 = bf16[4096,256]{0,1:T(8,128)(2,1)S(1)} fusion(bf16[4096,256]{0,1:T(8,128)(2,1)} %copy.55, f32[256,4096]{1,0:T(8,128)} %fusion.4, bf16[1,1,1536,4096]{3,2,1,0:T(8,128)(2,1)} %all-gather.8.cloned.1.call-done, bf16[1536,256]{0,1:T(8,128)(2,1)} %copy-done.3, f32[1536,256]{0,1:T(8,128)} %get-tuple-element.37, f32[1536]{0:T(1024)S(1)} %reduce_sum.100, ...), kind=kOutput, calls=%fused_computation.13 | convolution fusion | flops 3255566336 | bytes 23344128 | tf_op jit(solution)/shard_map/td,tf->df/dot_general | solution.py:105
  284.8 1.5 copy.79
  286.4 5.3 %all-to-all-start.2 = ((bf16[8,512,256]{1,2,0:T(8,128)(2,1)}), bf16[8,512,256]{1,2,0:T(8,128)(2,1)S(1)}, u32[]{:S(2)}, u32[]{:S(2)}) async-start(bf16[8,512,256]{1,2,0:T(8,128)(2,1)} %bitcast.114), calls=%async_computation.2 | async-start | bytes 4194304 | tf_op jit(solution)/shard_map/all_to_all | solution.py:61
  291.7 0.2 copy.65
  291.9 1.2 copy.64
  293.2 0.5 multiply_subtract_fusion.2
  293.7 24.2 %all-to-all-done.2 = bf16[8,512,256]{1,2,0:T(8,128)(2,1)S(1)} async-done(((bf16[8,512,256]{1,2,0:T(8,128)(2,1)}), bf16[8,512,256]{1,2,0:T(8,128)(2,1)S(1)}, u32[]{:S(2)}, u32[]{:S(2)}) %all-to-all-start.2) | async-done | bytes 2097184 | tf_op jit(solution)/shard_map/all_to_all | solution.py:61
  317.9 0.3 convert_reduce_fusion
  318.2 0.2 multiply_add_fusion
  318.4 1.0 copy.67
  319.4 1.0 copy.68
  (25 shorter events, 0.2 us)
Async XLA Ops:
  8.0 136.5 %all-reduce.3.cloned.1.call-start = ((), (), s32[]{:S(2)}) async-start(), calls=%async_computation.6 | async-start | bytes 4198400
  14.8 1.3 copy-start
  16.1 3.5 %copy-start.6 = (bf16[1,2,1536,256]{3,2,1,0:T(8,128)(2,1)S(1)}, bf16[1,2,1536,256]{3,2,1,0:T(8,128)(2,1)}, u32[]{:S(2)}) copy-start(bf16[1,2,1536,256]{3,2,1,0:T(8,128)(2,1)} %param.12) | copy-start | bytes 4718596
  16.1 142.1 %all-gather.6.cloned.1.call-start = ((), (), s32[]{:S(2)}) async-start(), calls=%async_computation.4 | async-start | bytes 13369344 | tf_op jit(solution)/shard_map/all_gather | solution.py:90
  19.0 201.2 %all-gather.8.cloned.1.call-start = ((), (), s32[]{:S(2)}) async-start(), calls=%async_computation.5 | async-start | bytes 13369344 | tf_op jit(solution)/shard_map/all_gather | solution.py:90
  193.4 2.1 copy-start.2
  195.5 0.9 copy-start.4
  197.1 12.1 %all-to-all-start = ((f32[16,1,1536]{2,1,0:T(1,128)}), f32[16,1,1536]{2,1,0:T(1,128)S(1)}, u32[]{:S(2)}, u32[]{:S(2)}) async-start(f32[16,1,1536]{2,1,0:T(1,128)} %broadcast_in_dim.4), calls=%async_computation | async-start | bytes 196608 | tf_op jit(solution)/shard_map/all_to_all | solution.py:45
  251.6 1.9 copy-start.1
  253.5 0.9 copy-start.3
  255.2 11.0 %all-to-all-start.1 = ((f32[16,1,1536]{2,1,0:T(1,128)}), f32[16,1,1536]{2,1,0:T(1,128)S(1)}, u32[]{:S(2)}, u32[]{:S(2)}) async-start(f32[16,1,1536]{2,1,0:T(1,128)} %broadcast_in_dim.5), calls=%async_computation.1 | async-start | bytes 196608 | tf_op jit(solution)/shard_map/all_to_all | solution.py:45
  266.2 20.2 %all-to-all-start.3 = ((bf16[8,1,32]{2,1,0:T(2,128)(2,1)}), bf16[8,1,32]{2,1,0:T(2,128)(2,1)S(1)}, u32[]{:S(2)}, u32[]{:S(2)}) async-start(bf16[8,1,32]{2,1,0:T(2,128)(2,1)} %copy.66), calls=%async_computation.3 | async-start | bytes 8192 | tf_op jit(solution)/shard_map/all_to_all | solution.py:61
  286.4 5.3 %copy-start.5 = (f32[512,256]{1,0:T(8,128)S(1)}, f32[512,256]{1,0:T(8,128)}, u32[]{:S(2)}) copy-start(f32[512,256]{1,0:T(8,128)} %param.7) | copy-start | bytes 1572868
  286.4 31.5 %all-to-all-start.2 = ((bf16[8,512,256]{1,2,0:T(8,128)(2,1)}), bf16[8,512,256]{1,2,0:T(8,128)(2,1)S(1)}, u32[]{:S(2)}, u32[]{:S(2)}) async-start(bf16[8,512,256]{1,2,0:T(8,128)(2,1)} %bitcast.114), calls=%async_computation.2 | async-start | bytes 4194304 | tf_op jit(solution)/shard_map/all_to_all | solution.py:61
  291.7 1.5 copy-start.7
  291.7 1.5 copy-start.8
Sparse Core Ops, SparseCore 0:
  16.2 128.2 all-reduce.2
Sparse Core Ops, SparseCore 1:
  19.1 95.1 all-gather.5
  116.5 88.7 all-gather.7
where the time goes:
time: 329 us; the launch traced here: 328 us
  waiting for transfers between devices  158 us (48%)
  matrix products  48.9 us (15%)
  blocking collectives  42.9 us (13%)
  local copies, waits for them, and re-layouts  35.1 us (11%)
  starting transfers between devices  18.1 us (6%)
  between operations  16.3 us (5%)
  other arithmetic  8.11 us (2%)
    unnamed x4, waiting for transfers between devices  120 us
    psum x6, blocking collectives, one_axis_at_a_time(): value = lax.psum(value, axis)  42.9 us
    dot_general x2, matrix products, per_device(): jnp.einsum('td,tf->df', rows_full, residual_grad, preferred_element_type=...  25.2 us
    all_to_all x2, waiting for transfers between devices, sent_and_summed(): lax.all_to_all(blocks, axis, split_axis=0, concat_axis=0, tiled=True)  24.2 us
    dot_general x2, matrix products, per_device(): jnp.dot(rows_full, weight_low, preferred_element_type=jnp.float32)  23.7 us
    all_to_all x2, waiting for transfers between devices, copy_for_each(): return lax.all_to_all(copies, axis, split_axis=0, concat_axis=0, tiled=True)  14 us
    unnamed x30, local copies, waits for them, and re-layouts  13.4 us
    all_to_all x2, starting transfers between devices, sent_and_summed(): lax.all_to_all(blocks, axis, split_axis=0, concat_axis=0, tiled=True)  9.57 us
  transfers between devices with their start and end apart: 7, of which 4 were waited for; matrix products, arithmetic and copies ran while one was open for 20% of the time, Pallas kernels for 0%

commit v1 on v0

--- a/solution.py
+++ b/solution.py
@@ -3,6 +3,7 @@
 from jax import lax
 from jax.sharding import Mesh
 from jax.sharding import PartitionSpec as P
+from jax.lax import all_gather
 
 D = 4096
 STEPS = 2
@@ -36,7 +37,7 @@
 
 def one_axis_at_a_time(value, axes):
     for axis in axes:
-        value = lax.psum(value, axis)
+        value = jnp.sum(all_gather(value, axis_name=axis), axis=0)
     return value
 
 

time: 329 us -> 332 us (level)
    all_gather x0 -> x6, blocking collectives: none -> 45 us  [one_axis_at_a_time(): value = jnp.sum(all_gather(value, axis_name=axis), axis=0)]
    psum x6 -> x0, blocking collectives: 42.9 us -> none  [one_axis_at_a_time(): value = lax.psum(value, axis)]
    unnamed x30 -> x36, local copies, waits for them, and re-layouts: 13.4 us -> 13.4 us
where the time goes in v1:
time: 332 us
  waiting for transfers between devices  158 us (48%)
  matrix products  48.9 us (15%)
  blocking collectives  45 us (14%)
  local copies, waits for them, and re-layouts  35.1 us (11%)
  starting transfers between devices  19.5 us (6%)
  between operations  16.4 us (5%)
  other arithmetic  8.27 us (2%)
    unnamed x4, waiting for transfers between devices  120 us
    all_gather x6, blocking collectives, one_axis_at_a_time(): value = jnp.sum(all_gather(value, axis_name=axis), axis=0)  45 us
    dot_general x2, matrix products, per_device(): jnp.einsum('td,tf->df', rows_full, residual_grad, preferred_element_type=...  25.2 us
    all_to_all x2, waiting for transfers between devices, sent_and_summed(): lax.all_to_all(blocks, axis, split_axis=0, concat_axis=0, tiled=True)  24.2 us
    dot_general x2, matrix products, per_device(): jnp.dot(rows_full, weight_low, preferred_element_type=jnp.float32)  23.7 us
    all_to_all x2, waiting for transfers between devices, copy_for_each(): return lax.all_to_all(copies, axis, split_axis=0, concat_axis=0, tiled=True)  14 us
    unnamed x36, local copies, waits for them, and re-layouts  13.4 us
    all_to_all x2, starting transfers between devices, copy_for_each(): return lax.all_to_all(copies, axis, split_axis=0, concat_axis=0, tiled=True)  10.3 us
  transfers between devices with their start and end apart: 7, of which 4 were waited for; matrix products, arithmetic and copies ran while one was open for 20% of the time, Pallas kernels for 0%

profile of v1, /device:TPU:1, one launch (start us, length us, event | category | flops | bytes accessed | tf_op | source)
XLA Modules:
  0.0 331.6 jit_solution(10572890856269305871)
XLA Ops:
  8.0 0.0 all-reduce.3.cloned.1.call-start
  8.0 1.1 convert_bitcast_fusion
  9.1 0.2 copy.77
  9.3 0.7 convert_element_type.86
  10.0 1.2 dynamic-slice
  11.9 0.2 broadcast.171
  12.1 2.6 dynamic-update-slice
  14.8 1.3 copy-done
  16.1 0.0 all-gather.18.cloned.1.call-start
  16.2 2.8 fusion.91
  19.0 0.0 all-gather.18.cloned.1.call-update
  19.0 0.0 all-gather.20.cloned.1.call-start
  19.0 0.5 all-gather.20.cloned.1.call-update
  19.6 0.1 fusion.90
  19.7 1.2 copy.72
  20.9 1.5 fusion.89
  22.3 1.2 copy.73
  23.5 1.2 copy.74
  24.7 0.3 copy.75
  24.9 119.6 %all-reduce.3.cloned.1.call-done = bf16[1048832]{0:T(1024)(128)(2,1)} async-done(((bf16[1048832]{0:T(1024)(128)(2,1)}), bf16[1048832]{0:T(1024)(128)(2,1)}) %all-reduce.3.cloned.1.call-update) | async-done | bytes 2097680
  144.5 4.1 %reshape.90 = bf16[8,131104]{1,0:T(8,128)(2,1)S(1)} reshape(bf16[1048832]{0:T(1024)(128)(2,1)} %all-reduce.3.cloned.1.call-done) | data formatting | bytes 4195328 | tf_op jit(solution)/shard_map/all_gather | solution.py:30
  148.6 1.4 slice.38
  150.0 3.9 %reshape_reshape.3 = bf16[4096,256]{1,0:T(8,128)(2,1)} reshape(bf16[8,131072]{1,0:T(8,128)(2,1)} %slice.38) | data formatting | bytes 4194304 | tf_op jit(solution)/shard_map/reshape;reshape | solution.py:25
  154.0 0.1 reshape.86
  154.0 4.2 %copy.55 = bf16[4096,256]{0,1:T(8,128)(2,1)} copy(bf16[4096,256]{1,0:T(8,128)(2,1)} %reshape_reshape.3) | data formatting | bytes 4194304 | tf_op jit(solution)/shard_map/reshape;reshape | solution.py:25
  158.2 10.2 %multiply_reduce_fusion.1 = (f32[1536]{0:T(1024)S(1)}, f32[1536,256]{0,1:T(8,128)}) fusion(bf16[4096,256]{1,0:T(8,128)(2,1)} %reshape_reshape.3, bf16[1,1,1536,4096]{3,2,1,0:T(8,128)(2,1)} %all-gather.18.cloned.1.call-done, bf16[1,1,1536,256]{2,3,1,0:T(8,128)(2,1)} %copy.72), kind=kOutput, calls=%fused_computation.56 | convolution fusion | flops 3223190016 | bytes 17045504 | tf_op jit(solution)/shard_map/dot_general | solution.py:93
  168.5 10.5 %all-gather.9 = f32[4,1,1536]{2,1,0:T(1,128)S(1)} all-gather(f32[1,1,1536]{2,1,0:T(1,128)S(1)} %reshape.102), channel_id=4, replica_groups=mesh['island'=8,'shard_0'=4,'shard_1'=2,'shard_2'=2] {'shard_0'}, dimensions={0}, use_global_device_ids=true | all-gather | bytes 30720 | tf_op jit(solution)/shard_map/all_gather | solution.py:40
  179.0 5.3 %all-gather.10 = f32[2,1,1536]{2,1,0:T(1,128)S(1)} all-gather(f32[1,1,1536]{2,1,0:T(1,128)S(1)} %reshape.104), channel_id=5, replica_groups=mesh['island'=8,'shard_0'=4,'shard_1'=2,'shard_2'=2] {'shard_1'}, dimensions={0}, use_global_device_ids=true | all-gather | bytes 18432 | tf_op jit(solution)/shard_map/all_gather | solution.py:40
  184.4 9.4 %all-gather.11 = f32[2,1,1536]{2,1,0:T(1,128)S(1)} all-gather(f32[1,1,1536]{2,1,0:T(1,128)S(1)} %reshape.106), channel_id=6, replica_groups=mesh['island'=8,'shard_0'=4,'shard_1'=2,'shard_2'=2] {'shard_2'}, dimensions={0}, use_global_device_ids=true | all-gather | bytes 18432 | tf_op jit(solution)/shard_map/all_gather | solution.py:40
  193.8 2.0 fusion.54
  195.8 0.1 copy-done.2
  195.9 0.6 fusion.50
  196.5 0.3 copy-done.4
  196.8 0.7 broadcast_in_dim.4
  197.5 6.7 %all-to-all-start = ((f32[16,1,1536]{2,1,0:T(1,128)}), f32[16,1,1536]{2,1,0:T(1,128)S(1)}, u32[]{:S(2)}, u32[]{:S(2)}) async-start(f32[16,1,1536]{2,1,0:T(1,128)} %broadcast_in_dim.4), calls=%async_computation | async-start | bytes 196608 | tf_op jit(solution)/shard_map/all_to_all | solution.py:46
  204.2 0.1 reduce_sum.162
  204.2 7.3 %all-to-all-done = f32[16,1,1536]{2,1,0:T(1,128)S(1)} async-done(((f32[16,1,1536]{2,1,0:T(1,128)}), f32[16,1,1536]{2,1,0:T(1,128)S(1)}, u32[]{:S(2)}, u32[]{:S(2)}) %all-to-all-start) | async-done | bytes 98336 | tf_op jit(solution)/shard_map/all_to_all | solution.py:46
  211.5 0.1 reduce_sum.153
  211.6 10.9 %fusion.4 = f32[256,4096]{1,0:T(8,128)} fusion(bf16[1,1,1536,4096]{3,2,1,0:T(8,128)(2,1)} %all-gather.18.cloned.1.call-done, bf16[1536,256]{0,1:T(8,128)(2,1)} %copy-done.4, f32[1536,256]{0,1:T(8,128)} %get-tuple-element.35, f32[1536]{0:T(1024)S(1)} %reduce_sum.153, f32[256]{0:T(256)S(1)} %reshape.86, f32[1536]{0:T(1024)S(1)} %add_rsqrt_fusion.1), kind=kOutput, calls=%fused_computation.4 | convolution fusion | flops 3225157632 | bytes 19149824 | tf_op jit(solution)/shard_map/td,tf->df/dot_general | solution.py:106
  222.5 13.5 %multiply_reduce_fusion = (f32[1536]{0:T(1024)S(1)}, f32[1536,256]{0,1:T(8,128)}) fusion(bf16[1,1,1536,4096]{3,2,1,0:T(8,128)(2,1)} %all-gather.20.cloned.1.call-done, f32[256,4096]{1,0:T(8,128)} %fusion.4, bf16[4096,256]{0,1:T(8,128)(2,1)} %copy.55, bf16[1,1,1536,256]{2,3,1,0:T(8,128)(2,1)} %copy.74), kind=kOutput, calls=%fused_computation.55 | convolution fusion | flops 3235772928 | bytes 21239808 | tf_op jit(solution)/shard_map/dot_general | solution.py:93
  236.0 9.1 %all-gather.12 = f32[4,1,1536]{2,1,0:T(1,128)S(1)} all-gather(f32[1,1,1536]{2,1,0:T(1,128)S(1)} %reshape.108), channel_id=8, replica_groups=mesh['island'=8,'shard_0'=4,'shard_1'=2,'shard_2'=2] {'shard_0'}, dimensions={0}, use_global_device_ids=true | all-gather | bytes 30720 | tf_op jit(solution)/shard_map/all_gather | solution.py:40
  245.1 4.7 %all-gather.13 = f32[2,1,1536]{2,1,0:T(1,128)S(1)} all-gather(f32[1,1,1536]{2,1,0:T(1,128)S(1)} %reshape.110), channel_id=9, replica_groups=mesh['island'=8,'shard_0'=4,'shard_1'=2,'shard_2'=2] {'shard_1'}, dimensions={0}, use_global_device_ids=true | all-gather | bytes 18432 | tf_op jit(solution)/shard_map/all_gather | solution.py:40
  249.8 6.1 %all-gather.14 = f32[2,1,1536]{2,1,0:T(1,128)S(1)} all-gather(f32[1,1,1536]{2,1,0:T(1,128)S(1)} %reshape.112), channel_id=10, replica_groups=mesh['island'=8,'shard_0'=4,'shard_1'=2,'shard_2'=2] {'shard_2'}, dimensions={0}, use_global_device_ids=true | all-gather | bytes 18432 | tf_op jit(solution)/shard_map/all_gather | solution.py:40
  256.0 1.8 fusion.53
  257.8 0.6 fusion.52
  258.5 0.2 copy-done.3
  258.7 0.1 reduce_sum.164
  258.8 0.7 broadcast_in_dim.5
  259.5 3.6 %all-to-all-start.1 = ((f32[16,1,1536]{2,1,0:T(1,128)}), f32[16,1,1536]{2,1,0:T(1,128)S(1)}, u32[]{:S(2)}, u32[]{:S(2)}) async-start(f32[16,1,1536]{2,1,0:T(1,128)} %broadcast_in_dim.5), calls=%async_computation.1 | async-start | bytes 196608 | tf_op jit(solution)/shard_map/all_to_all | solution.py:46
  263.1 0.6 copy.66
  263.7 6.8 %all-to-all-done.1 = f32[16,1,1536]{2,1,0:T(1,128)S(1)} async-done(((f32[16,1,1536]{2,1,0:T(1,128)}), f32[16,1,1536]{2,1,0:T(1,128)S(1)}, u32[]{:S(2)}, u32[]{:S(2)}) %all-to-all-start.1) | async-done | bytes 98336 | tf_op jit(solution)/shard_map/all_to_all | solution.py:46
  270.5 3.8 %all-to-all-start.3 = ((bf16[8,1,32]{2,1,0:T(2,128)(2,1)}), bf16[8,1,32]{2,1,0:T(2,128)(2,1)S(1)}, u32[]{:S(2)}, u32[]{:S(2)}) async-start(bf16[8,1,32]{2,1,0:T(2,128)(2,1)} %copy.66), calls=%async_computation.3 | async-start | bytes 8192 | tf_op jit(solution)/shard_map/all_to_all | solution.py:62
  274.3 0.1 reduce_sum.160
  274.4 14.3 %fusion.10 = bf16[4096,256]{0,1:T(8,128)(2,1)S(1)} fusion(bf16[4096,256]{0,1:T(8,128)(2,1)} %copy.55, f32[256,4096]{1,0:T(8,128)} %fusion.4, bf16[1,1,1536,4096]{3,2,1,0:T(8,128)(2,1)} %all-gather.20.cloned.1.call-done, bf16[1536,256]{0,1:T(8,128)(2,1)} %copy-done.3, f32[1536,256]{0,1:T(8,128)} %get-tuple-element.37, f32[1536]{0:T(1024)S(1)} %reduce_sum.160, ...), kind=kOutput, calls=%fused_computation.13 | convolution fusion | flops 3255566336 | bytes 23344128 | tf_op jit(solution)/shard_map/td,tf->df/dot_general | solution.py:106
  288.7 1.5 copy.79
  290.2 5.3 %all-to-all-start.2 = ((bf16[8,512,256]{1,2,0:T(8,128)(2,1)}), bf16[8,512,256]{1,2,0:T(8,128)(2,1)S(1)}, u32[]{:S(2)}, u32[]{:S(2)}) async-start(bf16[8,512,256]{1,2,0:T(8,128)(2,1)} %bitcast.114), calls=%async_computation.2 | async-start | bytes 4194304 | tf_op jit(solution)/shard_map/all_to_all | solution.py:62
  295.5 0.2 copy.65
  295.7 1.2 copy.64
  297.0 0.5 multiply_subtract_fusion.2
  297.5 24.2 %all-to-all-done.2 = bf16[8,512,256]{1,2,0:T(8,128)(2,1)S(1)} async-done(((bf16[8,512,256]{1,2,0:T(8,128)(2,1)}), bf16[8,512,256]{1,2,0:T(8,128)(2,1)S(1)}, u32[]{:S(2)}, u32[]{:S(2)}) %all-to-all-start.2) | async-done | bytes 2097184 | tf_op jit(solution)/shard_map/all_to_all | solution.py:62
  321.7 0.3 convert_reduce_fusion
  322.0 0.2 multiply_add_fusion
  322.2 1.0 copy.67
  323.2 1.0 copy.68
  (37 shorter events, 0.4 us)
Async XLA Ops:
  8.0 136.5 %all-reduce.3.cloned.1.call-start = ((), (), s32[]{:S(2)}) async-start(), calls=%async_computation.6 | async-start | bytes 4198400
  14.8 1.3 copy-start
  16.1 3.5 %copy-start.6 = (bf16[1,2,1536,256]{3,2,1,0:T(8,128)(2,1)S(1)}, bf16[1,2,1536,256]{3,2,1,0:T(8,128)(2,1)}, u32[]{:S(2)}) copy-start(bf16[1,2,1536,256]{3,2,1,0:T(8,128)(2,1)} %param.12) | copy-start | bytes 4718596
  16.1 142.1 %all-gather.18.cloned.1.call-start = ((), (), s32[]{:S(2)}) async-start(), calls=%async_computation.4 | async-start | bytes 13369344 | tf_op jit(solution)/shard_map/all_gather | solution.py:91
  19.0 203.5 %all-gather.20.cloned.1.call-start = ((), (), s32[]{:S(2)}) async-start(), calls=%async_computation.5 | async-start | bytes 13369344 | tf_op jit(solution)/shard_map/all_gather | solution.py:91
  193.8 2.1 copy-start.2
  195.9 0.9 copy-start.4
  197.5 14.0 %all-to-all-start = ((f32[16,1,1536]{2,1,0:T(1,128)}), f32[16,1,1536]{2,1,0:T(1,128)S(1)}, u32[]{:S(2)}, u32[]{:S(2)}) async-start(f32[16,1,1536]{2,1,0:T(1,128)} %broadcast_in_dim.4), calls=%async_computation | async-start | bytes 196608 | tf_op jit(solution)/shard_map/all_to_all | solution.py:46
  255.9 1.9 copy-start.1
  257.8 0.9 copy-start.3
  259.5 11.1 %all-to-all-start.1 = ((f32[16,1,1536]{2,1,0:T(1,128)}), f32[16,1,1536]{2,1,0:T(1,128)S(1)}, u32[]{:S(2)}, u32[]{:S(2)}) async-start(f32[16,1,1536]{2,1,0:T(1,128)} %broadcast_in_dim.5), calls=%async_computation.1 | async-start | bytes 196608 | tf_op jit(solution)/shard_map/all_to_all | solution.py:46
  270.5 19.7 %all-to-all-start.3 = ((bf16[8,1,32]{2,1,0:T(2,128)(2,1)}), bf16[8,1,32]{2,1,0:T(2,128)(2,1)S(1)}, u32[]{:S(2)}, u32[]{:S(2)}) async-start(bf16[8,1,32]{2,1,0:T(2,128)(2,1)} %copy.66), calls=%async_computation.3 | async-start | bytes 8192 | tf_op jit(solution)/shard_map/all_to_all | solution.py:62
  290.2 5.3 %copy-start.5 = (f32[512,256]{1,0:T(8,128)S(1)}, f32[512,256]{1,0:T(8,128)}, u32[]{:S(2)}) copy-start(f32[512,256]{1,0:T(8,128)} %param.7) | copy-start | bytes 1572868
  290.2 31.5 %all-to-all-start.2 = ((bf16[8,512,256]{1,2,0:T(8,128)(2,1)}), bf16[8,512,256]{1,2,0:T(8,128)(2,1)S(1)}, u32[]{:S(2)}, u32[]{:S(2)}) async-start(bf16[8,512,256]{1,2,0:T(8,128)(2,1)} %bitcast.114), calls=%async_computation.2 | async-start | bytes 4194304 | tf_op jit(solution)/shard_map/all_to_all | solution.py:62
  295.5 1.5 copy-start.7
  295.5 1.5 copy-start.8
Sparse Core Ops, SparseCore 0:
  16.2 128.2 all-reduce.2
Sparse Core Ops, SparseCore 1:
  19.1 95.1 all-gather.17
  116.5 88.6 all-gather.19
